TPU v7x, 32 devices: a whole 2x2x4 slice. The times are simulated.
32 devices in a mesh: site: 16 (over z, x, core), sec: 2 (over y).
Axes of the slice: x: 2, y: 2, z: 4, core: 2. Of those that a mesh axis runs over, the one named last changes fastest.
Arguments:
- left_canon: bfloat16 [16, 4, 4, 128, 128], P('site', None, 'sec'), may hold values from -1.5 to 1.5
- right_canon: bfloat16 [16, 4, 4, 128, 128], P('site', None, 'sec'), may hold values from -1.5 to 1.5
- center_site: bfloat16 [16, 4, 4, 128, 128], P('site', None, 'sec'), may hold values from -6 to 6
- center_bond: bfloat16 [16, 4, 128, 128], P('site', 'sec'), may hold values from -2 to 3
- left_seed: bfloat16 [16, 4, 128, 128], P('site', 'sec'), may hold values from -2 to 4
- right_seed: bfloat16 [16, 4, 128, 128], P('site', 'sec'), may hold values from -2 to 4
- left_sector: int32 [16, 4, 4], P('site'), may hold values from 0 to 3, each once within a row
- onsite: float32 [16, 4], P('site'), may hold values from 0.5 to 2
- bond_shift: float32 [16], P('site'), may hold values from 0.5 to 2
Outputs:
- left_new: bfloat16 [16, 4, 4, 128, 128], P('site', None, 'sec')
- right_new: bfloat16 [16, 4, 4, 128, 128], P('site', None, 'sec')
Inputs may be any that keep to these rules, and one draw needn't show every extreme that they name: `left_sector`: for each site and local state the 4 entries are a permutation of the sectors.
All inputs are finite; a program needn't handle non-finite values.
Results may differ from a plain program's by a relative error of at most 0.028.
Values may be sent and summed in bfloat16 or wider, within the bound.
No kernel may reach another device: no remote copies, remote signals or barrier semaphores. Data moves between devices by JAX's collectives and lax.ppermute only.
A program may use at most 64 MiB of HBM per device.

v0:
```python
import jax
import jax.numpy as jnp
from jax import lax
from jax.sharding import PartitionSpec as P

NSI = 10
NAPP = 2


def from_behind(block, axis, distance):
    devices = range(lax.axis_size(axis))
    route = [((i - distance) % len(devices), i) for i in devices]
    return lax.ppermute(block, axis, route)


def inverse_root(gram_mat):
    scaling = jnp.sqrt(jnp.sum(gram_mat * gram_mat, axis=(-2, -1), keepdims=True))
    identity = jnp.eye(gram_mat.shape[-1], dtype=jnp.float32)
    upper_part = gram_mat / scaling
    lower_part = jnp.broadcast_to(identity, gram_mat.shape)
    for repeat in range(NSI):
        middle = 1.5 * identity - 0.5 * jnp.matmul(
            lower_part, upper_part, precision=lax.Precision.HIGHEST
        )
        upper_part = jnp.matmul(upper_part, middle, precision=lax.Precision.HIGHEST)
        lower_part = jnp.matmul(middle, lower_part, precision=lax.Precision.HIGHEST)
    return lower_part / jnp.sqrt(scaling)


def trace_sum(blocks):
    return jnp.sum(jnp.diagonal(blocks.astype(jnp.float32), axis1=1, axis2=2))


def left_turn(hold_full, tensor_blocks, indices):
    running = jnp.zeros(tensor_blocks.shape[1:], jnp.float32)
    for physical in range(tensor_blocks.shape[0]):
        chosen = jnp.take(hold_full, indices[physical], axis=0)
        product = jnp.einsum(
            "kab,kbc->kac", chosen, tensor_blocks[physical], preferred_element_type=jnp.float32
        ).astype(jnp.bfloat16)
        running = running + jnp.einsum(
            "kba,kbc->kac", tensor_blocks[physical], product, preferred_element_type=jnp.float32
        )
    return running.astype(jnp.bfloat16)


def right_turn(hold_full, tensor_all, indices):
    running = jnp.zeros((indices.shape[1],) + hold_full.shape[1:], jnp.float32)
    for physical in range(tensor_all.shape[0]):
        picked = jnp.take(tensor_all[physical], indices[physical], axis=0)
        env_chosen = jnp.take(hold_full, indices[physical], axis=0)
        product = jnp.einsum(
            "kab,kbc->kac", picked, env_chosen, preferred_element_type=jnp.float32
        ).astype(jnp.bfloat16)
        running = running + jnp.einsum(
            "kac,kdc->kad", product, picked, preferred_element_type=jnp.float32
        )
    return running.astype(jnp.bfloat16)


def right_polar(gram_right, previous):
    gram_prev = jnp.einsum("kab,kcb->kac", previous, previous, preferred_element_type=jnp.float32)
    unit_right = jnp.matmul(
        inverse_root(gram_prev), previous.astype(jnp.float32), precision=lax.Precision.HIGHEST
    )
    return jnp.matmul(
        jnp.swapaxes(unit_right, -1, -2), inverse_root(gram_right), precision=lax.Precision.HIGHEST
    ).astype(jnp.bfloat16)


def per_device(
    left_canon,
    right_canon,
    center_site,
    center_bond,
    left_seed,
    right_seed,
    left_sector,
    onsite,
    bond_shift,
):
    canon_left = left_canon[0]
    canon_right = right_canon[0]
    site_now = center_site[0]
    bond_now = center_bond[0]
    sources = left_sector[0]
    energy = onsite[0]
    bond_add = bond_shift[0]
    owned = canon_left.shape[1]
    width = canon_left.shape[2]
    sectors = sources.shape[1]
    offset = lax.axis_index("sec") * owned
    labels = jnp.arange(sectors, dtype=jnp.int32)
    right_of = jnp.sum(
        jnp.where(sources[:, :, None] == labels[None, None, :], labels[None, :, None], 0), axis=1
    )
    own_sources = lax.dynamic_slice_in_dim(sources, offset, owned, 1)
    steps_total = lax.axis_size("site") // 4
    dim_all = sectors * width
    all_left, all_right, left_start, right_start = (
        lax.all_gather(canon_left, "sec", axis=1, tiled=True),
        lax.all_gather(canon_right, "sec", axis=1, tiled=True),
        lax.all_gather(left_seed[0], "sec", axis=0, tiled=True),
        lax.all_gather(right_seed[0], "sec", axis=0, tiled=True),
    )

    def chain_turn(count_now, state_tuple):
        left_hold, right_hold, left_last = state_tuple
        left_fresh = left_turn(left_hold, all_left, sources)
        right_fresh = right_turn(right_hold, all_right, right_of)
        left_moved = from_behind(left_fresh, "site", 1)
        right_moved = from_behind(right_fresh, "site", -1)
        return (left_moved, right_moved, left_fresh)

    env_cur, env_right, env_next = lax.fori_loop(
        0, steps_total, chain_turn, (left_start, right_start, left_start)
    )
    trace_cur = trace_sum(env_cur)
    trace_next = trace_sum(env_next)
    trace_right = trace_sum(env_right)
    next_own = lax.dynamic_slice_in_dim(env_next, offset, owned, 0)
    right_own = lax.dynamic_slice_in_dim(env_right, offset, owned, 0)
    cur_scaled = (env_cur.astype(jnp.float32) * (dim_all / trace_cur)).astype(jnp.bfloat16)
    next_scaled = (next_own.astype(jnp.float32) * (dim_all / trace_next)).astype(jnp.bfloat16)
    right_scaled = (right_own.astype(jnp.float32) * (dim_all / trace_right)).astype(jnp.bfloat16)
    chosen_left = jnp.take(cur_scaled, own_sources, axis=0)
    for repeat in range(NAPP):
        half_site = jnp.einsum(
            "skab,skbc->skac", chosen_left, site_now, preferred_element_type=jnp.float32
        ).astype(jnp.bfloat16)
        site_now = (
            jnp.einsum(
                "skab,kbc->skac", half_site, right_scaled, preferred_element_type=jnp.float32
            )
            + energy[:, None, None, None] * site_now.astype(jnp.float32)
        ).astype(jnp.bfloat16)
        half_bond = jnp.einsum(
            "kab,kbc->kac", next_scaled, bond_now, preferred_element_type=jnp.float32
        ).astype(jnp.bfloat16)
        bond_now = (
            jnp.einsum("kab,kbc->kac", half_bond, right_scaled, preferred_element_type=jnp.float32)
            + bond_add * bond_now.astype(jnp.float32)
        ).astype(jnp.bfloat16)
    gram_left = jnp.einsum("skab,skac->kbc", site_now, site_now, preferred_element_type=jnp.float32)
    gram_bond = jnp.einsum("kab,kac->kbc", bond_now, bond_now, preferred_element_type=jnp.float32)
    unit_left = jnp.matmul(
        bond_now.astype(jnp.float32), inverse_root(gram_bond), precision=lax.Precision.HIGHEST
    )
    factor_left = jnp.matmul(
        inverse_root(gram_left), jnp.swapaxes(unit_left, -1, -2), precision=lax.Precision.HIGHEST
    ).astype(jnp.bfloat16)
    left_new = jnp.einsum(
        "skab,kbc->skac", site_now, factor_left, preferred_element_type=jnp.float32
    ).astype(jnp.bfloat16)
    outer_terms = jnp.einsum(
        "skab,skcb->skac", site_now, site_now, preferred_element_type=jnp.float32
    )
    routing = (own_sources[:, :, None] == labels[None, None, :]).astype(jnp.float32)
    buffer_all = jnp.einsum("skm,skac->mac", routing, outer_terms, precision=lax.Precision.HIGHEST)
    previous = from_behind(bond_now, "site", 1)
    gram_part = lax.psum_scatter(buffer_all, "sec", scatter_dimension=0, tiled=True)
    factor_part = right_polar(gram_part, previous)
    factor_right = lax.all_gather(factor_part, "sec", axis=0, tiled=True)
    factor_chosen = jnp.take(factor_right, own_sources, axis=0)
    right_new = jnp.einsum(
        "skab,skbc->skac", factor_chosen, site_now, preferred_element_type=jnp.float32
    ).astype(jnp.bfloat16)
    return (left_new[None], right_new[None])


def solution(mesh):
    return jax.shard_map(
        per_device,
        mesh=mesh,
        in_specs=(
            P("site", None, "sec", None, None),
            P("site", None, "sec", None, None),
            P("site", None, "sec", None, None),
            P("site", "sec", None, None),
            P("site", "sec", None, None),
            P("site", "sec", None, None),
            P("site", None, None),
            P("site", None),
            P("site"),
        ),
        out_specs=(P("site", None, "sec", None, None), P("site", None, "sec", None, None)),
        check_vma=False,
    )
```

profile of v0, /device:TPU:0, one launch (start us, length us, event | category | flops | bytes accessed | tf_op | source)
XLA Modules:
  0.0 190.5 jit_solution(11089584762305972886)
XLA Ops:
  7.2 0.8 select_reduce_fusion
  8.0 10.2 %all-gather.3 = bf16[1,4,4,128,128]{4,3,2,1,0:T(8,128)(2,1)S(1)} all-gather(bf16[1,4,2,128,128]{4,3,2,1,0:T(8,128)(2,1)} %param.16), channel_id=5, replica_groups=mesh['site'=16,'sec'=2] {'sec'}, dimensions={2}, use_global_device_ids=true | all-gather | bytes 786432 | tf_op jit(solution)/shard_map/all_gather | solution.py:102
  18.3 5.1 %all-gather = bf16[1,4,128,128]{3,2,0,1:T(8,128)(2,1)S(1)} all-gather(bf16[1,2,128,128]{3,2,0,1:T(8,128)(2,1)} %bitcast.414), channel_id=2, replica_groups=mesh['site'=16,'sec'=2] {'sec'}, dimensions={1}, use_global_device_ids=true | all-gather | bytes 196608 | tf_op jit(solution)/shard_map/all_gather | solution.py:103
  23.6 0.7 copy.260
  24.3 7.2 %all-gather.2 = bf16[1,4,4,128,128]{4,3,2,1,0:T(8,128)(2,1)S(1)} all-gather(bf16[1,4,2,128,128]{4,3,2,1,0:T(8,128)(2,1)} %param.15), channel_id=4, replica_groups=mesh['site'=16,'sec'=2] {'sec'}, dimensions={2}, use_global_device_ids=true | all-gather | bytes 786432 | tf_op jit(solution)/shard_map/all_gather | solution.py:101
  31.5 5.1 %all-gather.1 = bf16[1,4,128,128]{3,2,0,1:T(8,128)(2,1)S(1)} all-gather(bf16[1,2,128,128]{3,2,0,1:T(8,128)(2,1)} %bitcast.415), channel_id=3, replica_groups=mesh['site'=16,'sec'=2] {'sec'}, dimensions={1}, use_global_device_ids=true | all-gather | bytes 196608 | tf_op jit(solution)/shard_map/all_gather | solution.py:104
  37.2 0.6 gather_fusion.12
  37.8 0.6 gather_fusion.13
  38.4 0.6 gather_fusion.14
  39.2 68.1 %while.16 = (s32[]{:T(128)}, bf16[4,128,128]{1,2,0:T(8,128)(2,1)S(1)}, bf16[4,128,128]{2,1,0:T(8,128)(2,1)S(1)}, bf16[4,128,128]{1,2,0:T(8,128)(2,1)}, s32[4,4]{...) while((s32[]{:T(128)}, ...), condition=%wide.region_2.0_spmd, body=%wide.region_1.3_spmd.sunk | while | flops 270016704 | bytes 9734929 | solution.py:115
  39.2 0.6 gather_fusion.4
  39.8 0.6 gather_fusion.5
  40.4 0.6 gather_fusion.6
  41.0 0.6 gather_fusion.7
  43.7 0.8 compare_and_fusion.15
  44.6 0.6 gather_fusion
  45.1 0.6 gather_fusion.1
  45.7 0.6 gather_fusion.2
  46.3 0.6 gather_fusion.3
  49.5 7.0 %collective-permute-done = bf16[4,128,128]{1,2,0:T(8,128)(2,1)S(1)} collective-permute-done((bf16[4,128,128]{1,2,0:T(8,128)(2,1)S(1)}, bf16[4,128,128]{1,2,0:T(8,128)(2,1)S(1)}, u32[]{:S(2)}, u32[]{:S(2)}) %collective-permute-start) | collective-permute-done | bytes 131104 | tf_op jit(solution)/shard_map/while/body/eval_jaxpr/ppermute | solution.py:13
  56.5 0.6 gather_fusion.4
  57.1 0.6 gather_fusion.5
  57.7 0.6 gather_fusion.6
  58.3 0.6 gather_fusion.7
  61.0 0.8 compare_and_fusion.15
  61.8 0.6 gather_fusion
  62.4 0.6 gather_fusion.1
  63.0 0.6 gather_fusion.2
  63.6 0.6 gather_fusion.3
  66.8 6.6 %collective-permute-done = bf16[4,128,128]{1,2,0:T(8,128)(2,1)S(1)} collective-permute-done((bf16[4,128,128]{1,2,0:T(8,128)(2,1)S(1)}, bf16[4,128,128]{1,2,0:T(8,128)(2,1)S(1)}, u32[]{:S(2)}, u32[]{:S(2)}) %collective-permute-start) | collective-permute-done | bytes 131104 | tf_op jit(solution)/shard_map/while/body/eval_jaxpr/ppermute | solution.py:13
  73.4 0.6 gather_fusion.4
  74.0 0.6 gather_fusion.5
  74.6 0.6 gather_fusion.6
  75.2 0.6 gather_fusion.7
  77.9 0.8 compare_and_fusion.15
  78.8 0.6 gather_fusion
  79.3 0.6 gather_fusion.1
  79.9 0.6 gather_fusion.2
  80.5 0.6 gather_fusion.3
  83.7 6.6 %collective-permute-done = bf16[4,128,128]{1,2,0:T(8,128)(2,1)S(1)} collective-permute-done((bf16[4,128,128]{1,2,0:T(8,128)(2,1)S(1)}, bf16[4,128,128]{1,2,0:T(8,128)(2,1)S(1)}, u32[]{:S(2)}, u32[]{:S(2)}) %collective-permute-start) | collective-permute-done | bytes 131104 | tf_op jit(solution)/shard_map/while/body/eval_jaxpr/ppermute | solution.py:13
  90.3 0.6 gather_fusion.4
  90.9 0.6 gather_fusion.5
  91.5 0.6 gather_fusion.6
  94.8 0.8 compare_and_fusion.15
  100.6 6.6 %collective-permute-done = bf16[4,128,128]{1,2,0:T(8,128)(2,1)S(1)} collective-permute-done((bf16[4,128,128]{1,2,0:T(8,128)(2,1)S(1)}, bf16[4,128,128]{1,2,0:T(8,128)(2,1)S(1)}, u32[]{:S(2)}, u32[]{:S(2)}) %collective-permute-start) | collective-permute-done | bytes 131104 | tf_op jit(solution)/shard_map/while/body/eval_jaxpr/ppermute | solution.py:13
  107.2 4.2 %copy.176 = f32[4,128,128]{0,2,1:T(8,128)} copy(bf16[4,128,128]{2,1,0:T(8,128)(2,1)S(1)} %get-tuple-element.113) | data formatting | bytes 393216 | tf_op jit(solution)/shard_map/convert_element_type | solution.py:31
  111.9 4.2 %copy.180 = f32[4,128,128]{0,2,1:T(8,128)} copy(bf16[4,128,128]{2,1,0:T(8,128)(2,1)S(1)} %copy.179) | data formatting | bytes 393216 | tf_op jit(solution)/shard_map/convert_element_type | solution.py:123
  116.0 1.8 gather_fusion.9
  117.8 0.6 reduce_sum.74
  119.4 1.8 gather_fusion.8
  121.1 0.6 reduce_sum.73
  122.7 0.6 gather_fusion.15
  124.6 0.9 convolution_bitcast_fusion.2
  125.5 0.7 copy.199
  126.3 7.3 %copy.189 = f32[4,128,128]{0,2,1:T(8,128)} copy(bf16[4,128,128]{1,2,0:T(8,128)(2,1)S(1)} %copy-done.1) | data formatting | bytes 393216 | tf_op jit(solution)/shard_map/convert_element_type | solution.py:31
  133.7 1.8 gather_fusion.10
  135.5 0.6 reduce_sum.76
  156.1 1.1 copy.203
  165.9 1.0 multiply_reduce_fusion
  166.9 1.3 fusion.100
  168.4 1.2 fusion.168
  177.1 4.9 %all_gather.19 = bf16[4,128,128]{2,1,0:T(8,128)(2,1)S(1)} all-gather(bf16[2,128,128]{2,1,0:T(8,128)(2,1)S(1)} %convolution_convert_fusion.12), channel_id=1, replica_groups=mesh['site'=16,'sec'=2] {'sec'}, dimensions={0}, use_global_device_ids=true | all-gather | bytes 196608 | tf_op jit(solution)/shard_map/all_gather | solution.py:163
  182.0 0.6 gather_fusion.16
  182.6 1.1 fusion.89
  (249 shorter events, 59.3 us)
Async XLA Ops:
  7.2 158.7 %reduce-scatter.2.cloned.1.call-start = ((), (), s32[]{:S(2)}) async-start(), calls=%async_computation.1 | async-start | bytes 393216 | tf_op jit(solution)/shard_map/reduce_scatter | solution.py:161
  43.6 5.9 %collective-permute-start.1 = (bf16[4,128,128]{2,1,0:T(8,128)(2,1)S(1)}, bf16[4,128,128]{2,1,0:T(8,128)(2,1)S(1)}, u32[]{:S(2)}, u32[]{:S(2)}) collective-permute-start(bf16[4,128,128]{2,1,0:T(8,128)(2,1)S(1)} %fusion.543), channel_id=1, source_target_pairs={{2,0},{4,2},{6,4},{8,6},{10,8},{12,10},{14,12},{16,14},{18,16},{20... | collective-permute-start | bytes 393224 | tf_op jit(solution)/shard_map/while/body/eval_jaxpr/ppermute | solution.py:13
  49.0 7.5 %copy-start = (bf16[4,128,128]{1,2,0:T(8,128)(2,1)}, bf16[4,128,128]{1,2,0:T(8,128)(2,1)S(1)}, u32[]{:S(2)}) copy-start(bf16[4,128,128]{1,2,0:T(8,128)(2,1)S(1)} %fusion.541) | copy-start | bytes 393220 | tf_op jit(solution)/shard_map/while
  49.0 7.5 %collective-permute-start = (bf16[4,128,128]{1,2,0:T(8,128)(2,1)S(1)}, bf16[4,128,128]{1,2,0:T(8,128)(2,1)S(1)}, u32[]{:S(2)}, u32[]{:S(2)}) collective-permute-start(bf16[4,128,128]{1,2,0:T(8,128)(2,1)S(1)} %fusion.541), channel_id=1, source_target_pairs={{30,0},{0,2},{2,4},{4,6},{6,8},{8,10},{10,12},{12,14},{14,16},{16,... | collective-permute-start | bytes 393224 | tf_op jit(solution)/shard_map/while/body/eval_jaxpr/ppermute | solution.py:13
  60.9 5.9 %collective-permute-start.1 = (bf16[4,128,128]{2,1,0:T(8,128)(2,1)S(1)}, bf16[4,128,128]{2,1,0:T(8,128)(2,1)S(1)}, u32[]{:S(2)}, u32[]{:S(2)}) collective-permute-start(bf16[4,128,128]{2,1,0:T(8,128)(2,1)S(1)} %fusion.543), channel_id=1, source_target_pairs={{2,0},{4,2},{6,4},{8,6},{10,8},{12,10},{14,12},{16,14},{18,16},{20... | collective-permute-start | bytes 393224 | tf_op jit(solution)/shard_map/while/body/eval_jaxpr/ppermute | solution.py:13
  66.2 7.2 %copy-start = (bf16[4,128,128]{1,2,0:T(8,128)(2,1)}, bf16[4,128,128]{1,2,0:T(8,128)(2,1)S(1)}, u32[]{:S(2)}) copy-start(bf16[4,128,128]{1,2,0:T(8,128)(2,1)S(1)} %fusion.541) | copy-start | bytes 393220 | tf_op jit(solution)/shard_map/while
  66.2 7.1 %collective-permute-start = (bf16[4,128,128]{1,2,0:T(8,128)(2,1)S(1)}, bf16[4,128,128]{1,2,0:T(8,128)(2,1)S(1)}, u32[]{:S(2)}, u32[]{:S(2)}) collective-permute-start(bf16[4,128,128]{1,2,0:T(8,128)(2,1)S(1)} %fusion.541), channel_id=1, source_target_pairs={{30,0},{0,2},{2,4},{4,6},{6,8},{8,10},{10,12},{12,14},{14,16},{16,... | collective-permute-start | bytes 393224 | tf_op jit(solution)/shard_map/while/body/eval_jaxpr/ppermute | solution.py:13
  77.8 5.9 %collective-permute-start.1 = (bf16[4,128,128]{2,1,0:T(8,128)(2,1)S(1)}, bf16[4,128,128]{2,1,0:T(8,128)(2,1)S(1)}, u32[]{:S(2)}, u32[]{:S(2)}) collective-permute-start(bf16[4,128,128]{2,1,0:T(8,128)(2,1)S(1)} %fusion.543), channel_id=1, source_target_pairs={{2,0},{4,2},{6,4},{8,6},{10,8},{12,10},{14,12},{16,14},{18,16},{20... | collective-permute-start | bytes 393224 | tf_op jit(solution)/shard_map/while/body/eval_jaxpr/ppermute | solution.py:13
  83.2 7.2 %copy-start = (bf16[4,128,128]{1,2,0:T(8,128)(2,1)}, bf16[4,128,128]{1,2,0:T(8,128)(2,1)S(1)}, u32[]{:S(2)}) copy-start(bf16[4,128,128]{1,2,0:T(8,128)(2,1)S(1)} %fusion.541) | copy-start | bytes 393220 | tf_op jit(solution)/shard_map/while
  83.2 7.1 %collective-permute-start = (bf16[4,128,128]{1,2,0:T(8,128)(2,1)S(1)}, bf16[4,128,128]{1,2,0:T(8,128)(2,1)S(1)}, u32[]{:S(2)}, u32[]{:S(2)}) collective-permute-start(bf16[4,128,128]{1,2,0:T(8,128)(2,1)S(1)} %fusion.541), channel_id=1, source_target_pairs={{30,0},{0,2},{2,4},{4,6},{6,8},{8,10},{10,12},{12,14},{14,16},{16,... | collective-permute-start | bytes 393224 | tf_op jit(solution)/shard_map/while/body/eval_jaxpr/ppermute | solution.py:13
  94.8 5.9 %collective-permute-start.1 = (bf16[4,128,128]{2,1,0:T(8,128)(2,1)S(1)}, bf16[4,128,128]{2,1,0:T(8,128)(2,1)S(1)}, u32[]{:S(2)}, u32[]{:S(2)}) collective-permute-start(bf16[4,128,128]{2,1,0:T(8,128)(2,1)S(1)} %fusion.543), channel_id=1, source_target_pairs={{2,0},{4,2},{6,4},{8,6},{10,8},{12,10},{14,12},{16,14},{18,16},{20... | collective-permute-start | bytes 393224 | tf_op jit(solution)/shard_map/while/body/eval_jaxpr/ppermute | solution.py:13
  100.1 7.2 %copy-start = (bf16[4,128,128]{1,2,0:T(8,128)(2,1)}, bf16[4,128,128]{1,2,0:T(8,128)(2,1)S(1)}, u32[]{:S(2)}) copy-start(bf16[4,128,128]{1,2,0:T(8,128)(2,1)S(1)} %fusion.541) | copy-start | bytes 393220 | tf_op jit(solution)/shard_map/while
  100.1 7.1 %collective-permute-start = (bf16[4,128,128]{1,2,0:T(8,128)(2,1)S(1)}, bf16[4,128,128]{1,2,0:T(8,128)(2,1)S(1)}, u32[]{:S(2)}, u32[]{:S(2)}) collective-permute-start(bf16[4,128,128]{1,2,0:T(8,128)(2,1)S(1)} %fusion.541), channel_id=1, source_target_pairs={{30,0},{0,2},{2,4},{4,6},{6,8},{8,10},{10,12},{12,14},{14,16},{16,... | collective-permute-start | bytes 393224 | tf_op jit(solution)/shard_map/while/body/eval_jaxpr/ppermute | solution.py:13
  107.2 4.3 %copy-start.3 = (s32[4,4]{1,0:T(4,128)S(1)}, s32[4,4]{1,0:T(4,128)}, u32[]{:S(2)}) copy-start(s32[4,4]{1,0:T(4,128)} %get-tuple-element.412) | copy-start | bytes 196
  107.2 15.3 %copy-start.2 = (bf16[1,4,2,128,128]{4,3,2,1,0:T(8,128)(2,1)S(1)}, bf16[1,4,2,128,128]{4,3,2,1,0:T(8,128)(2,1)}, u32[]{:S(2)}) copy-start(bf16[1,4,2,128,128]{4,3,2,1,0:T(8,128)(2,1)} %param.17) | copy-start | bytes 786436
  107.2 16.1 %copy-start.5 = (f32[1,4]{1,0:T(1,128)S(1)}, f32[1,4]{1,0:T(1,128)}, u32[]{:S(2)}) copy-start(f32[1,4]{1,0:T(1,128)} %param.22) | copy-start | bytes 52
  111.4 14.8 %copy-start.1 = (bf16[4,128,128]{1,2,0:T(8,128)(2,1)S(1)}, bf16[4,128,128]{1,2,0:T(8,128)(2,1)}, u32[]{:S(2)}) copy-start(bf16[4,128,128]{1,2,0:T(8,128)(2,1)} %get-tuple-element.115) | copy-start | bytes 393220
  116.0 21.4 %copy-start.4 = (bf16[1,2,128,128]{3,2,1,0:T(8,128)(2,1)S(1)}, bf16[1,2,128,128]{3,2,1,0:T(8,128)(2,1)}, u32[]{:S(2)}) copy-start(bf16[1,2,128,128]{3,2,1,0:T(8,128)(2,1)} %param.18) | copy-start | bytes 196612
  138.0 19.1 %collective-permute-start.2 = (bf16[2,128,128]{2,1,0:T(8,128)(2,1)S(1)}, bf16[2,128,128]{2,1,0:T(8,128)(2,1)S(1)}, u32[]{:S(2)}, u32[]{:S(2)}) collective-permute-start(bf16[2,128,128]{2,1,0:T(8,128)(2,1)S(1)} %fusion.132), channel_id=1, source_target_pairs={{30,0},{0,2},{2,4},{4,6},{6,8},{8,10},{10,12},{12,14},{14,16},{16,... | collective-permute-start | bytes 196616 | tf_op jit(solution)/shard_map/ppermute | solution.py:13
Sparse Core Ops, SparseCore 0:
  126.4 9.0 reduce-scatter.1
where the time goes:
time: 191 us
  matrix products  55.8 us (29%)
  local copies, waits for them, and re-layouts  46.5 us (24%)
  blocking collectives  32.7 us (17%)
  waiting for transfers between devices  26.8 us (14%)
  between operations  18 us (9%)
  other arithmetic  7.46 us (4%)
  starting transfers between devices  2.68 us (1%)
    ppermute x9, waiting for transfers between devices, from_behind(): return lax.ppermute(block, axis, route)  26.7 us
    dot_general x40, matrix products, inverse_root(): jnp.matmul(lower_part, upper_part, precision=lax.Precision.HIGHEST)  12 us
    convert_element_type x2, local copies, waits for them, and re-layouts, trace_sum(): return jnp.sum(jnp.diagonal(blocks.astype(jnp.float32), axis1=1, axis2=2))  11.5 us
    dot_general x36, matrix products, inverse_root(): upper_part = jnp.matmul(upper_part, middle, precision=lax.Precision.HIGHEST)  10.7 us
    dot_general x40, matrix products, inverse_root(): lower_part = jnp.matmul(middle, lower_part, precision=lax.Precision.HIGHEST)  10.7 us
    all_gather x1, blocking collectives, per_device(): lax.all_gather(canon_right, 'sec', axis=1, tiled=True)  10.2 us
    gather x16, local copies, waits for them, and re-layouts, left_turn(): chosen = jnp.take(hold_full, indices[physical], axis=0)  9.15 us
    gather x16, local copies, waits for them, and re-layouts, right_turn(): env_chosen = jnp.take(hold_full, indices[physical], axis=0)  9.15 us
  transfers between devices with their start and end apart: 10, of which 4 were waited for; matrix products, arithmetic and copies ran while one was open for 30% of the time, Pallas kernels for 0%

commit v1 on v0

v1 whole, which is shorter than its diff:
```python
import functools

import jax
import jax.numpy as jnp
from jax import lax
from jax.experimental import pallas as pl
from jax.experimental.pallas import tpu as pltpu
from jax.sharding import PartitionSpec as P

NSI = 10
NAPP = 2
f32 = jnp.float32
bf16 = jnp.bfloat16
VMEM = pl.BlockSpec(memory_space=pltpu.VMEM)
SMEM = pl.BlockSpec(memory_space=pltpu.SMEM)
ANY = pl.BlockSpec(memory_space=pl.ANY)


def dot(a, b):
    return jnp.dot(a, b, preferred_element_type=f32)


def dot_tn(a, b):
    return lax.dot_general(a, b, (((0,), (0,)), ((), ())), preferred_element_type=f32)


def dot_nt(a, b):
    return lax.dot_general(a, b, (((1,), (1,)), ((), ())), preferred_element_type=f32)


def split(x):
    high = x.astype(bf16)
    low = (x - high.astype(f32)).astype(bf16)
    return jnp.concatenate([high, low], axis=1)


def twice(s):
    return jnp.concatenate([s, s], axis=0)


def fold(x):
    width = x.shape[1] // 2
    return x[:, :width] + x[:, width:]


def eye(width):
    rows = lax.broadcasted_iota(jnp.int32, (width, width), 0)
    cols = lax.broadcasted_iota(jnp.int32, (width, width), 1)
    return (rows == cols).astype(f32)


def total(x):
    return jnp.sum(jnp.sum(x, axis=0, keepdims=True), axis=1, keepdims=True)


class Table:
    def __init__(self, ref, phys, n):
        self.ref, self.phys, self.n = ref, phys, n

    def src(self, g, s, k):
        return self.ref[((g * 2) * self.phys + s) * self.n + k]

    def dst(self, g, s, m):
        return self.ref[((g * 2 + 1) * self.phys + s) * self.n + m]


def gather_states(blocks, table, g, m, phys):
    return jnp.concatenate([blocks[s, table.dst(g, s, m)] for s in range(phys)], axis=1)


def scatter_states(store, product, table, g, m, phys, width):
    for s in range(phys):
        store[table.dst(g, s, m), s * width : (s + 1) * width, :] = product[
            :, s * width : (s + 1) * width
        ]


def chain_kernel(dims, first, last, tab_ref, pos_ref, *refs):
    hops, sizes, phys, n, own, width = dims
    count = hops * sizes
    local_left, local_right = refs[0], refs[1]
    moved = (None,) + refs[2 : 2 + count - 1]
    rest = refs[2 + count - 1 :]
    if not first:
        env_in, rest = rest[0], rest[1:]
    elif hops == 1:
        seeds, rest = rest[:2], rest[2:]
    out_ref, blocks, env, wide, tall, sems = rest
    table = Table(tab_ref, phys, n)
    pos = pos_ref[0]

    def slot(t):
        return pl.ds(lax.rem(pos - t + sizes, sizes) * own, own)

    def copies(local):
        found = []
        for g in range(hops):
            for t in range(sizes):
                i = g * sizes + t
                source = local if i == 0 else moved[i].at[pl.ds(0, phys)]
                found.append(
                    pltpu.make_async_copy(source, blocks.at[g, :, slot(t)], sems.at[i])
                )
        return found

    def seed_copies(local):
        found = []
        for t in range(sizes):
            i = (hops - 1) * sizes + t
            source = local if i == 0 else moved[i].at[phys]
            found.append(pltpu.make_async_copy(source, env.at[slot(t)], sems.at[count + t]))
        return found

    def run(local, seed, step):
        loads = copies(local)
        starts = seed_copies(seed) if first else []
        for copy in starts + loads:
            copy.start()
        if not first:
            env[...] = env_in[...]
        for copy in starts:
            copy.wait()
        for g in reversed(range(hops)):
            for copy in loads[g * sizes : (g + 1) * sizes]:
                copy.wait()
            step(g)

    def left_step(g):
        for m in range(n):
            product = dot(env[m], gather_states(blocks.at[g], table, g, m, phys)).astype(bf16)
            scatter_states(tall, product, table, g, m, phys, width)
        for k in range(n):
            stacked = blocks[g, :, k].reshape(phys * width, width)
            env[k] = dot_tn(stacked, tall[k]).astype(bf16)

    def right_step(g):
        for k in range(n):
            stacked = blocks[g, :, k].reshape(phys * width, width)
            product = dot(stacked, env[k]).astype(bf16)
            for s in range(phys):
                wide[table.src(g, s, k), :, s * width : (s + 1) * width] = product[
                    s * width : (s + 1) * width
                ]
        for m in range(n):
            env[m] = dot_nt(wide[m], gather_states(blocks.at[g], table, g, m, phys)).astype(bf16)

    local_seeds = seeds if first and hops == 1 else (None, None)

    @pl.when(pos < sizes // 2)
    def _():
        run(local_left, local_seeds[0], left_step)

    @pl.when(pos >= sizes // 2)
    def _():
        run(local_right, local_seeds[1], right_step)

    if last:
        summed = env[0].astype(f32)
        for m in range(1, n):
            summed = summed + env[m].astype(f32)
        scale = (n * width) / total(summed * eye(width))
        for m in range(n):
            out_ref[m] = (env[m].astype(f32) * scale).astype(bf16)
    else:
        out_ref[...] = env[...]


def center_kernel(dims, tab_ref, pos_ref, onsite_ref, shift_ref, *refs):
    sizes, phys, n, own, width = dims
    same_ref, cross_ref, mine_ref, swap_ref, bond_ref = refs[:5]
    site_parts = refs[5 : 5 + sizes]
    bond_parts = refs[5 + sizes : 5 + 2 * sizes]
    left_out, right_out = refs[5 + 2 * sizes : 7 + 2 * sizes]
    site, envs, bonds, tall, y_ref, z_ref, m_ref, scale_ref, factor_ref, sems = refs[
        7 + 2 * sizes :
    ]
    table = Table(tab_ref, phys, n)
    pos = pos_ref[0]
    on_right = (pos >= sizes // 2).astype(jnp.int32)

    def slot(t, extra=0):
        return pl.ds(extra + lax.rem(pos - t + sizes, sizes) * own, own)

    copies = []
    for t in range(sizes):
        copies.append(
            pltpu.make_async_copy(site_parts[t], site.at[:, slot(t)], sems.at[t])
        )
        copies.append(
            pltpu.make_async_copy(bond_parts[t], bonds.at[slot(t, own)], sems.at[sizes + t])
        )
    targets = (
        (same_ref, on_right),
        (cross_ref, 1 - on_right),
        (mine_ref, 3 - on_right),
        (swap_ref, 2 + on_right),
    )
    for i, (ref, where) in enumerate(targets):
        copies.append(pltpu.make_async_copy(ref, envs.at[where], sems.at[2 * sizes + i]))
    for copy in copies:
        copy.start()
    bonds[0:own] = bond_ref[...]
    for copy in copies:
        copy.wait()

    for repeat in range(NAPP):
        for m in range(n):
            product = dot(envs[0, m], gather_states(site, table, 0, m, phys)).astype(bf16)
            scatter_states(tall, product, table, 0, m, phys, width)
        for i in range(own):
            k = pos * own + i
            half = dot(envs[3, k], bonds[i]).astype(bf16)
            bonds[i] = (dot(half, envs[1, k]) + shift_ref[0] * bonds[i].astype(f32)).astype(bf16)
        for m in range(n):
            half = dot(envs[0, m], bonds[own + m]).astype(bf16)
            bonds[own + m] = (
                dot(half, envs[2, m]) + shift_ref[1] * bonds[own + m].astype(f32)
            ).astype(bf16)
        for k in range(n):
            product = dot(tall[k], envs[1, k])
            for s in range(phys):
                site[s, k] = (
                    product[s * width : (s + 1) * width] + onsite_ref[s] * site[s, k].astype(f32)
                ).astype(bf16)

    count = 2 * (own + n)

    def gram(i):
        if i < own + n:
            return dot_nt(bonds[i], bonds[i])
        i -= own + n
        if i < own:
            stacked = site[:, pos * own + i].reshape(phys * width, width)
            return dot_tn(stacked, stacked)
        gathered = gather_states(site, table, 0, i - own, phys)
        return dot_nt(gathered, gathered)

    for i in range(count):
        g = gram(i)
        inverse = lax.rsqrt(total(g * g))
        scale_ref[i] = jnp.broadcast_to(jnp.sqrt(inverse), scale_ref.shape[1:])
        y = g * inverse
        y_ref[i] = split(y)
        z_ref[i] = split(1.5 * eye(width) - 0.5 * y)
    for i in range(count):
        y_ref[i] = split(fold(dot(z_ref[i], twice(y_ref[i]))))

    def middle():
        for i in range(count):
            m_ref[i] = split(1.5 * eye(width) - 0.5 * fold(dot(z_ref[i], twice(y_ref[i]))))

    def finish():
        for i in range(count):
            z_ref[i] = split(fold(dot(m_ref[i], twice(z_ref[i]))))

    def iterate(step, carry):
        middle()
        for i in range(count):
            y_ref[i] = split(fold(dot(m_ref[i], twice(y_ref[i]))))
        finish()
        return carry

    lax.fori_loop(0, NSI - 2, iterate, 0)
    middle()
    finish()

    for i in range(own + n):
        unit = dot(z_ref[i], twice(bonds[i])) * scale_ref[i][:1]
        y_ref[i] = split(unit)
    for i in range(own + n):
        grams = own + n + i
        parts = y_ref[i]
        if i < own:
            high, low = parts[:, :width], parts[:, width:]
            rows = jnp.concatenate(
                [
                    jnp.concatenate([high, high], axis=1),
                    jnp.concatenate([low, low], axis=1),
                ],
                axis=0,
            )
            factor = fold(dot_nt(z_ref[grams], rows)) * scale_ref[grams][:1]
        else:
            factor = jnp.transpose(fold(dot(z_ref[grams], twice(parts))) * scale_ref[grams][:1])
        factor_ref[i] = factor.astype(bf16)
    for i in range(own):
        k = pos * own + i
        stacked = site[:, k].reshape(phys * width, width)
        product = dot(stacked, factor_ref[i]).astype(bf16)
        for s in range(phys):
            left_out[s, i] = product[s * width : (s + 1) * width]
            right_out[s, i] = dot(factor_ref[own + table.src(0, s, k)], site[s, k]).astype(bf16)


def route(mesh_shape, target):
    sites, sizes = mesh_shape
    pairs = []
    for j in range(sites):
        for c in range(sizes):
            to = target(j, c)
            if to is not None:
                pairs.append((j * sizes + c, (to[0] % sites) * sizes + to[1] % sizes))
    return pairs


def per_device(
    mesh_shape,
    left_canon,
    right_canon,
    center_site,
    center_bond,
    left_seed,
    right_seed,
    left_sector,
    onsite,
    bond_shift,
):
    sites, sizes = mesh_shape
    half = sizes // 2
    steps = sites // 4
    hops = 2 if steps % 2 == 0 else 1
    left, right = left_canon[0], right_canon[0]
    phys, own, width = left.shape[0], left.shape[1], left.shape[2]
    src = left_sector[0]
    n = src.shape[1]
    labels = jnp.arange(n, dtype=jnp.int32)
    dst = jnp.sum(
        jnp.where(src[:, :, None] == labels[None, None, :], labels[None, :, None], 0), axis=1
    )
    tab = jnp.stack([src, dst]).reshape(-1)
    pos = lax.axis_index("sec").astype(jnp.int32)
    params = pltpu.CompilerParams(vmem_limit_bytes=56 * 2**20)

    def move(x, target):
        return lax.ppermute(x, ("site", "sec"), route(mesh_shape, target))

    def outward(c, g):
        return g if c < half else -g

    moved, tables = [], [tab]
    for g in range(hops):
        for t in range(sizes):
            if g == 0 and t == 0:
                continue
            to_left = lax.rem(pos + t, sizes) < half
            payload = jnp.where(to_left, left, right)
            if g == hops - 1:
                seed = jnp.where(to_left, left_seed[0], right_seed[0])
                payload = jnp.concatenate([payload, seed[None]], axis=0)
            moved.append(
                move(payload, lambda j, c, g=g, t=t: (j + outward((c + t) % sizes, g), c + t))
            )
        if g > 0:
            tables.append(move(tab, lambda j, c, g=g: (j + outward(c, g), c)))
    tables = jnp.concatenate(tables)
    shift_before = move(bond_shift, lambda j, c: (j + 1, c))

    dims = (hops, sizes, phys, n, own, width)
    env_shape = jax.ShapeDtypeStruct((n, width, width), bf16)
    count = hops * sizes
    env = None
    blocks_total = steps // hops
    for b in range(blocks_total):
        first, last = b == 0, b == blocks_total - 1
        extra, specs = (), []
        if not first:
            extra, specs = (env,), [VMEM]
        elif hops == 1:
            extra, specs = (left_seed[0], right_seed[0]), [ANY, ANY]
        env = pl.pallas_call(
            functools.partial(chain_kernel, dims, first, last),
            out_shape=env_shape,
            in_specs=[SMEM, SMEM] + [ANY] * (count + 1) + specs,
            out_specs=VMEM,
            scratch_shapes=[
                pltpu.VMEM((hops, phys, n, width, width), bf16),
                pltpu.VMEM((n, width, width), bf16),
                pltpu.VMEM((n, width, phys * width), bf16),
                pltpu.VMEM((n, phys * width, width), bf16),
                pltpu.SemaphoreType.DMA((count + sizes,)),
            ],
            compiler_params=params,
            name="chain_last" if last else "chain",
        )(tables, pos[None], left, right, *moved, *extra)
        if first:
            center, bond, _ = lax.optimization_barrier((center_site[0], center_bond[0], env))
            center_parts = [center_site[0]] + [
                move(center, lambda j, c, t=t: (j, c + t)) for t in range(1, sizes)
            ]
            bond_parts = [move(bond, lambda j, c, t=t: (j + 1, c + t)) for t in range(sizes)]
        if not last:
            env = move(env, lambda j, c: (j + outward(c, hops), c))

    same = move(env, lambda j, c: (j + outward(c, 1), c))
    cross = move(env, lambda j, c: (j + outward(c, 1), c + half))
    swap = move(env, lambda j, c: (j, c + half))

    matrices = 2 * (own + n)
    out_shape = jax.ShapeDtypeStruct((phys, own, width, width), bf16)
    left_new, right_new = pl.pallas_call(
        functools.partial(center_kernel, (sizes, phys, n, own, width)),
        out_shape=(out_shape, out_shape),
        in_specs=[SMEM] * 4 + [ANY] * 4 + [VMEM] + [ANY] * (2 * sizes),
        out_specs=(VMEM, VMEM),
        scratch_shapes=[
            pltpu.VMEM((phys, n, width, width), bf16),
            pltpu.VMEM((4, n, width, width), bf16),
            pltpu.VMEM((own + n, width, width), bf16),
            pltpu.VMEM((n, phys * width, width), bf16),
            pltpu.VMEM((matrices, width, 2 * width), bf16),
            pltpu.VMEM((matrices, width, 2 * width), bf16),
            pltpu.VMEM((matrices, width, 2 * width), bf16),
            pltpu.VMEM((matrices, 8, width), f32),
            pltpu.VMEM((own + n, width, width), bf16),
            pltpu.SemaphoreType.DMA((2 * sizes + 4,)),
        ],
        compiler_params=params,
        name="center",
    )(
        tab,
        pos[None],
        onsite[0],
        jnp.concatenate([bond_shift, shift_before]),
        same,
        cross,
        env,
        swap,
        center_bond[0],
        *center_parts,
        *bond_parts,
    )
    return (left_new[None], right_new[None])


def solution(mesh):
    mesh_shape = (mesh.shape["site"], mesh.shape["sec"])
    return jax.shard_map(
        functools.partial(per_device, mesh_shape),
        mesh=mesh,
        in_specs=(
            P("site", None, "sec", None, None),
            P("site", None, "sec", None, None),
            P("site", None, "sec", None, None),
            P("site", "sec", None, None),
            P("site", "sec", None, None),
            P("site", "sec", None, None),
            P("site", None, None),
            P("site", None),
            P("site"),
        ),
        out_specs=(P("site", None, "sec", None, None), P("site", None, "sec", None, None)),
        check_vma=False,
    )
```

time: 191 us -> 61.8 us (0.32)
  matrix products: 55.8 us -> 0 us
  local copies, waits for them, and re-layouts: 46.5 us -> 3.06 us
  blocking collectives: 32.7 us -> 0 us
  Pallas kernels: 0 us -> 20.8 us
  between operations: 18 us -> 1.49 us
  starting transfers between devices: 2.68 us -> 13.7 us
  waiting for transfers between devices: 26.8 us -> 18.5 us
  other arithmetic: 7.46 us -> 3.19 us
    dot_general x163 -> x0, matrix products: 55.8 us -> none  [the longest x40 12 us: inverse_root(): jnp.matmul(lower_part, upper_part, precision=lax.Precision.HIGHEST)]
    all_gather x5 -> x0, blocking collectives: 32.7 us -> none  [the longest x1 10.2 us: per_device(): lax.all_gather(canon_right, 'sec', axis=1, tiled=True)]
    gather x41 -> x0, local copies, waits for them, and re-layouts: 27.1 us -> none  [the longest x16 9.15 us: left_turn(): chosen = jnp.take(hold_full, indices[physical], axis=0)]
    pallas_call x0 -> x3, Pallas kernels: none -> 20.8 us  [the longest x1 12.8 us: per_device(): pl.pallas_call(functools.partial(center_kernel, (sizes, phys, n, own, wid...]
    convert_element_type x3 -> x0, local copies, waits for them, and re-layouts: 15.6 us -> none  [the longest x2 11.5 us: trace_sum(): return jnp.sum(jnp.diagonal(blocks.astype(jnp.float32), axis1=1, axis2=2))]
    ppermute x9 -> x12, starting transfers between devices: 2.65 us -> 13.7 us  [move(): return lax.ppermute(x, ('site', 'sec'), route(mesh_shape, target))]
    ppermute x9 -> x12, waiting for transfers between devices: 26.7 us -> 18.5 us  [move(): return lax.ppermute(x, ('site', 'sec'), route(mesh_shape, target))]
    reduce_sum x5 -> x1, other arithmetic: 3.64 us -> 0.09 us  [per_device(): jnp.sum(jnp.where(src[:, :, None] == labels[None, None, :], labels[None,...]
  transfers between devices with their start and end apart: 10 -> 12, of which waited for: 4 -> 3; matrix products, arithmetic and copies ran while one was open for 30% -> 4% of each run, Pallas kernels for 0% -> 7%
where the time goes in v1:
time: 61.8 us; the launch traced here: 60.8 us
  Pallas kernels  20.8 us (34%)
  waiting for transfers between devices  18.5 us (30%)
  starting transfers between devices  13.7 us (22%)
  other arithmetic  3.19 us (5%)
  local copies, waits for them, and re-layouts  3.06 us (5%)
  between operations  1.49 us (2%)
    ppermute x12, waiting for transfers between devices, move(): return lax.ppermute(x, ('site', 'sec'), route(mesh_shape, target))  18.5 us
    ppermute x12, starting transfers between devices, move(): return lax.ppermute(x, ('site', 'sec'), route(mesh_shape, target))  13.7 us
    pallas_call x1, Pallas kernels, per_device(): pl.pallas_call(functools.partial(center_kernel, (sizes, phys, n, own, wid...  12.8 us
    pallas_call x2, Pallas kernels, per_device(): pl.pallas_call(functools.partial(chain_kernel, dims, first, last), out_sh...  8.07 us
    unnamed x32, local copies, waits for them, and re-layouts  2.97 us
    concatenate x1, other arithmetic, per_device(): jnp.concatenate([bond_shift, shift_before])  1.27 us
  transfers between devices with their start and end apart: 12, of which 3 were waited for; matrix products, arithmetic and copies ran while one was open for 4% of the time, Pallas kernels for 7%

profile of v1, /device:TPU:0, one launch (start us, length us, event | category | flops | bytes accessed | tf_op | source)
XLA Modules:
  0.0 60.8 jit_solution(7460469315076916371)
XLA Ops:
  0.6 0.0 copy-start.12
  0.6 0.0 copy-start.13
  0.7 1.1 %broadcast_select_fusion = (bf16[4,2,128,128]{3,2,1,0:T(8,128)(2,1)S(1)}, bf16[4,2,128,128]{3,2,1,0:T(8,128)(2,1)S(1)}) fusion(pred[]{:T(512)S(6)} %lt.8, bf16[1,4,2,128,128]{4,3,2,1,0:T(8,128)(2,1)} %param.10, bf16[1,4,2,128,128]{4,3,2,1,0:T(8,128)(2,1)} %param.9, pred[]{:T(512)S(6)} %lt.7), kind=kLoop, calls=%fused_computation.2 | loop fusion | flops 262144 | bytes 1048578 | tf_op jit(solution)/shard_map/jit(_where)/select_n | solution.py:346
  1.8 3.1 %collective-permute-start.2 = (bf16[4,2,128,128]{3,2,1,0:T(8,128)(2,1)S(1)}, bf16[4,2,128,128]{3,2,1,0:T(8,128)(2,1)S(1)}, u32[]{:S(2)}, u32[]{:S(2)}) collective-permute-start(bf16[4,2,128,128]{3,2,1,0:T(8,128)(2,1)S(1)} %get-tuple-element.11), channel_id=1, source_target_pairs={{0,1},{1,0},{2,3},{3,2},{4,5},{5,4},{6,7},{7,6},{8,9},{9,8},{10,11... | collective-permute-start | bytes 786440 | tf_op jit(solution)/shard_map/ppermute | solution.py:335
  4.8 0.0 copy-done.12
  4.8 0.0 copy-done.13
  4.9 3.7 %collective-permute-start.4 = (bf16[5,2,128,128]{3,2,1,0:T(8,128)(2,1)S(1)}, bf16[5,2,128,128]{3,2,1,0:T(8,128)(2,1)S(1)}, u32[]{:S(2)}, u32[]{:S(2)}) collective-permute-start(bf16[5,2,128,128]{3,2,1,0:T(8,128)(2,1)S(1)} %pad_maximum_fusion.1), channel_id=1, source_target_pairs={{0,31},{1,2},{2,1},{3,4},{4,3},{5,6},{6,5},{7,8},{8,7},{9,10},{10,... | collective-permute-start | bytes 983048 | tf_op jit(solution)/shard_map/ppermute | solution.py:335
  8.6 0.0 copy-start.14
  8.6 0.1 collective-permute-start.3
  8.7 0.6 copy-done.14
  9.3 0.1 select_reduce_fusion
  9.4 0.1 reshape.8.tab_ref
  9.5 0.0 copy-start.15
  9.5 0.0 collective-permute-start.1
  9.5 8.5 %collective-permute-done.1 = s32[32]{0:T(128)S(1)} collective-permute-done((s32[32]{0:T(128)S(1)}, s32[32]{0:T(128)S(1)}, u32[]{:S(2)}, u32[]{:S(2)}) %collective-permute-start.1) | collective-permute-done | bytes 160 | tf_op jit(solution)/shard_map/ppermute | solution.py:335
  18.0 0.7 %pad_add_fusion.1.tab_ref = s32[64]{0:T(128)} fusion(s32[32]{0:T(128)S(1)} %collective-permute-done.1, s32[32]{0:T(128)S(1)} %reshape.8.tab_ref), kind=kLoop, calls=%fused_computation.10 | loop fusion | flops 64 | bytes 512 | tf_op jit(solution)/shard_map/concatenate | solution.py:355
  18.6 0.0 copy-done.15
  18.6 0.0 collective-permute-done.2.refs_2_
  18.6 0.0 copy-start.2
  18.6 0.0 collective-permute-done.4.refs_4_
  18.6 0.0 copy-start
  18.6 0.0 collective-permute-done.3.refs_3_
  18.6 0.0 copy-start.1
  18.7 0.7 %copy-done.2 = bf16[4,2,128,128]{3,2,1,0:T(8,128)(2,1)} copy-done((bf16[4,2,128,128]{3,2,1,0:T(8,128)(2,1)}, bf16[4,2,128,128]{3,2,1,0:T(8,128)(2,1)S(1)}, u32[]{:S(2)}) %copy-start.2) | copy-done | bytes 262168
  19.3 0.1 copy-done
  19.4 0.1 copy-done.1
  19.5 0.0 copy-start.3
  19.5 0.0 copy-start.9
  19.6 4.0 %chain.1 = bf16[4,128,128]{2,1,0:T(8,128)(2,1)} custom-call(s32[64]{0:T(128)} %pad_add_fusion.1.tab_ref, s32[1]{0:T(128)} %bitcast.2.pos_ref, bf16[4,2,128,128]{3,2,1,0:T(8,128)(2,1)} %bitcast.14, bf16[4,2,128,128]{3,2,1,0:T(8,128)(2,1)} %bitcast.16, bf16[4,2,128,128]{3,2,1,0:T(8,128)(2,1)} %copy-done.2, bf16[5,2,128,128]{3,2,1,0:T(8,128)(2,1)} %copy-done.1, ...), custom_call_target="tpu_custom_call" | custom-call | tf_op jit(solution)/shard_map/chain/pallas_call | solution.py:370
  23.5 0.1 collective-permute-start.5
  23.6 0.0 copy-done.3
  23.6 5.7 %collective-permute-start.9 = (bf16[4,2,128,128]{3,2,1,0:T(8,128)(2,1)S(1)}, bf16[4,2,128,128]{3,2,1,0:T(8,128)(2,1)S(1)}, u32[]{:S(2)}, u32[]{:S(2)}) collective-permute-start(bf16[4,2,128,128]{3,2,1,0:T(8,128)(2,1)S(1)} %bitcast.19), channel_id=1, source_target_pairs={{0,1},{1,0},{2,3},{3,2},{4,5},{5,4},{6,7},{7,6},{8,9},{9,8},{10,11... | collective-permute-start | bytes 786440 | tf_op jit(solution)/shard_map/ppermute | solution.py:335
  29.3 0.0 copy-done.9
  29.3 0.0 collective-permute-start.11
  29.3 0.0 collective-permute-start
  29.3 2.2 %collective-permute-done.5.refs_5_ = bf16[4,128,128]{2,1,0:T(8,128)(2,1)S(1)} collective-permute-done((bf16[4,128,128]{2,1,0:T(8,128)(2,1)}, bf16[4,128,128]{2,1,0:T(8,128)(2,1)S(1)}, u32[]{:S(2)}, u32[]{:S(2)}) %collective-permute-start.5) | collective-permute-done | bytes 131104 | tf_op jit(solution)/shard_map/ppermute | solution.py:335
  31.5 0.0 copy-start.8
  31.5 0.7 %copy-done.8 = bf16[4,128,128]{2,1,0:T(8,128)(2,1)} copy-done((bf16[4,128,128]{2,1,0:T(8,128)(2,1)}, bf16[4,128,128]{2,1,0:T(8,128)(2,1)S(1)}, u32[]{:S(2)}) %copy-start.8) | copy-done | bytes 131096
  32.1 4.1 %chain_last.1.refs_2_ = bf16[4,128,128]{2,1,0:T(8,128)(2,1)} custom-call(s32[64]{0:T(128)} %pad_add_fusion.1.tab_ref, s32[1]{0:T(128)} %bitcast.2.pos_ref, bf16[4,2,128,128]{3,2,1,0:T(8,128)(2,1)} %bitcast.15, bf16[4,2,128,128]{3,2,1,0:T(8,128)(2,1)} %bitcast.17, bf16[4,2,128,128]{3,2,1,0:T(8,128)(2,1)} %copy-done.2, bf16[5,2,128,128]{3,2,1,0:T(8,128)(2,1)} %copy-done.1, ...), custom_call_target="tpu_custom_call" | custom-call | tf_op jit(solution)/shard_map/chain_last/pallas_call | solution.py:370
  36.2 0.7 %collective-permute-start.8 = (bf16[4,128,128]{2,1,0:T(8,128)(2,1)}, bf16[4,128,128]{2,1,0:T(8,128)(2,1)S(1)}, u32[]{:S(2)}, u32[]{:S(2)}) collective-permute-start(bf16[4,128,128]{2,1,0:T(8,128)(2,1)} %chain_last.1.refs_2_), channel_id=1, source_target_pairs={{0,1},{1,0},{2,3},{3,2},{4,5},{5,4},{6,7},{7,6},{8,9},{9,8},{10,11... | collective-permute-start | bytes 393224 | tf_op jit(solution)/shard_map/ppermute | solution.py:335
  36.9 0.0 collective-permute-start.7
  36.9 0.0 collective-permute-done
  36.9 0.0 collective-permute-start.6
  37.6 0.0 collective-permute-done.11.refs_8_
  37.6 0.0 copy-start.10
  37.6 0.5 collective-permute-start.10
  38.1 1.3 %pad_maximum_fusion.2.shift_ref = f32[2]{0:T(128)} fusion(f32[1]{0:T(128)} %collective-permute-done, f32[1]{0:T(128)S(6)} %copy.11), kind=kLoop, calls=%fused_computation.9 | loop fusion | flops 2 | bytes 16 | tf_op jit(solution)/shard_map/concatenate | solution.py:423
  39.3 7.8 %collective-permute-done.10.refs_7_ = bf16[2,128,128]{2,1,0:T(8,128)(2,1)S(1)} collective-permute-done((bf16[2,128,128]{2,1,0:T(8,128)(2,1)S(1)}, bf16[2,128,128]{2,1,0:T(8,128)(2,1)S(1)}, u32[]{:S(2)}, u32[]{:S(2)}) %collective-permute-start.10) | collective-permute-done | bytes 65568 | tf_op jit(solution)/shard_map/ppermute | solution.py:335
  47.2 0.0 copy-start.11
  47.2 0.0 collective-permute-done.9.refs_6_
  47.2 0.0 copy-start.4
  47.2 0.0 collective-permute-done.8.refs_3_
  47.2 0.0 copy-start.5
  47.2 0.0 collective-permute-done.7.refs_1_
  47.2 0.0 copy-start.6
  47.2 0.0 collective-permute-done.6.refs_0_
  47.2 0.0 copy-start.7
  47.2 0.0 copy-done.10
  47.3 0.5 copy-done.11
  47.8 0.1 copy-done.4
  47.9 0.0 copy-done.5
  48.0 0.1 copy-done.6
  48.0 0.1 copy-done.7
  48.1 12.8 %center.1 = (bf16[4,2,128,128]{3,2,1,0:T(8,128)(2,1)}, bf16[4,2,128,128]{3,2,1,0:T(8,128)(2,1)}) custom-call(s32[32]{0:T(128)} %copy-done.15, s32[1]{0:T(128)} %bitcast.2.pos_ref, f32[4]{0:T(128)} %bitcast.25, f32[2]{0:T(128)} %pad_maximum_fusion.2.shift_ref, bf16[4,128,128]{2,1,0:T(8,128)(2,1)} %copy-done.7, bf16[4,128,128]{2,1,0:T(8,128)(2,1)} %copy-done.6, ...), custom_call_target="tpu_custom_call" | custom-call | tf_op jit(solution)/shard_map/center/pallas_call | solution.py:400
  (4 shorter events, 0.1 us)
Async XLA Ops:
  0.6 4.2 %copy-start.12 = (bf16[1,2,128,128]{3,2,1,0:T(8,128)(2,1)S(1)}, bf16[1,2,128,128]{3,2,1,0:T(8,128)(2,1)}, u32[]{:S(2)}) copy-start(bf16[1,2,128,128]{3,2,1,0:T(8,128)(2,1)} %param.13) | copy-start | bytes 196612
  0.6 4.2 %copy-start.13 = (bf16[1,2,128,128]{3,2,1,0:T(8,128)(2,1)S(1)}, bf16[1,2,128,128]{3,2,1,0:T(8,128)(2,1)}, u32[]{:S(2)}) copy-start(bf16[1,2,128,128]{3,2,1,0:T(8,128)(2,1)} %param.14) | copy-start | bytes 196612
  1.8 16.9 %collective-permute-start.2 = (bf16[4,2,128,128]{3,2,1,0:T(8,128)(2,1)S(1)}, bf16[4,2,128,128]{3,2,1,0:T(8,128)(2,1)S(1)}, u32[]{:S(2)}, u32[]{:S(2)}) collective-permute-start(bf16[4,2,128,128]{3,2,1,0:T(8,128)(2,1)S(1)} %get-tuple-element.11), channel_id=1, source_target_pairs={{0,1},{1,0},{2,3},{3,2},{4,5},{5,4},{6,7},{7,6},{8,9},{9,8},{10,11... | collective-permute-start | bytes 786440 | tf_op jit(solution)/shard_map/ppermute | solution.py:335
  4.9 13.7 %collective-permute-start.4 = (bf16[5,2,128,128]{3,2,1,0:T(8,128)(2,1)S(1)}, bf16[5,2,128,128]{3,2,1,0:T(8,128)(2,1)S(1)}, u32[]{:S(2)}, u32[]{:S(2)}) collective-permute-start(bf16[5,2,128,128]{3,2,1,0:T(8,128)(2,1)S(1)} %pad_maximum_fusion.1), channel_id=1, source_target_pairs={{0,31},{1,2},{2,1},{3,4},{4,3},{5,6},{6,5},{7,8},{8,7},{9,10},{10,... | collective-permute-start | bytes 983048 | tf_op jit(solution)/shard_map/ppermute | solution.py:335
  8.6 0.7 %copy-start.14 = (s32[1,4,4]{2,1,0:T(4,128)S(1)}, s32[1,4,4]{2,1,0:T(4,128)}, u32[]{:S(2)}) copy-start(s32[1,4,4]{2,1,0:T(4,128)} %param.15) | copy-start | bytes 196
  8.6 10.0 %collective-permute-start.3 = (bf16[5,2,128,128]{3,2,1,0:T(8,128)(2,1)S(1)}, bf16[5,2,128,128]{3,2,1,0:T(8,128)(2,1)S(1)}, u32[]{:S(2)}, u32[]{:S(2)}) collective-permute-start(bf16[5,2,128,128]{3,2,1,0:T(8,128)(2,1)S(1)} %pad_maximum_fusion), channel_id=1, source_target_pairs={{0,2},{1,31},{2,4},{3,1},{4,6},{5,3},{6,8},{7,5},{8,10},{9,7},{10,... | collective-permute-start | bytes 983048 | tf_op jit(solution)/shard_map/ppermute | solution.py:335
  9.5 9.2 %copy-start.15 = (s32[32]{0:T(128)}, s32[32]{0:T(128)S(1)}, u32[]{:S(2)}) copy-start(s32[32]{0:T(128)S(1)} %reshape.8.tab_ref) | copy-start | bytes 388
  9.5 8.5 %collective-permute-start.1 = (s32[32]{0:T(128)S(1)}, s32[32]{0:T(128)S(1)}, u32[]{:S(2)}, u32[]{:S(2)}) collective-permute-start(s32[32]{0:T(128)S(1)} %reshape.8.tab_ref), channel_id=1, source_target_pairs={{0,2},{1,31},{2,4},{3,1},{4,6},{5,3},{6,8},{7,5},{8,10},{9,7},{10,... | collective-permute-start | bytes 392 | tf_op jit(solution)/shard_map/ppermute | solution.py:335
  18.6 0.7 %copy-start.2 = (bf16[4,2,128,128]{3,2,1,0:T(8,128)(2,1)}, bf16[4,2,128,128]{3,2,1,0:T(8,128)(2,1)S(1)}, u32[]{:S(2)}) copy-start(bf16[4,2,128,128]{3,2,1,0:T(8,128)(2,1)S(1)} %collective-permute-done.2.refs_2_) | copy-start | bytes 786436
  18.6 0.8 %copy-start = (bf16[5,2,128,128]{3,2,1,0:T(8,128)(2,1)}, bf16[5,2,128,128]{3,2,1,0:T(8,128)(2,1)S(1)}, u32[]{:S(2)}) copy-start(bf16[5,2,128,128]{3,2,1,0:T(8,128)(2,1)S(1)} %collective-permute-done.4.refs_4_) | copy-start | bytes 983044
  18.6 0.9 %copy-start.1 = (bf16[5,2,128,128]{3,2,1,0:T(8,128)(2,1)}, bf16[5,2,128,128]{3,2,1,0:T(8,128)(2,1)S(1)}, u32[]{:S(2)}) copy-start(bf16[5,2,128,128]{3,2,1,0:T(8,128)(2,1)S(1)} %collective-permute-done.3.refs_3_) | copy-start | bytes 983044
  19.5 4.0 %copy-start.3 = (bf16[1,4,2,128,128]{4,3,2,1,0:T(8,128)(2,1)S(1)}, bf16[1,4,2,128,128]{4,3,2,1,0:T(8,128)(2,1)}, u32[]{:S(2)}) copy-start(bf16[1,4,2,128,128]{4,3,2,1,0:T(8,128)(2,1)} %param.11) | copy-start | bytes 786436
  19.5 9.7 %copy-start.9 = (bf16[1,2,128,128]{3,2,1,0:T(8,128)(2,1)S(1)}, bf16[1,2,128,128]{3,2,1,0:T(8,128)(2,1)}, u32[]{:S(2)}) copy-start(bf16[1,2,128,128]{3,2,1,0:T(8,128)(2,1)} %param.12) | copy-start | bytes 196612
  23.5 8.0 %collective-permute-start.5 = (bf16[4,128,128]{2,1,0:T(8,128)(2,1)}, bf16[4,128,128]{2,1,0:T(8,128)(2,1)S(1)}, u32[]{:S(2)}, u32[]{:S(2)}) collective-permute-start(bf16[4,128,128]{2,1,0:T(8,128)(2,1)} %chain.1), channel_id=1, source_target_pairs={{0,4},{1,29},{2,6},{3,31},{4,8},{5,1},{6,10},{7,3},{8,12},{9,5},{1... | collective-permute-start | bytes 393224 | tf_op jit(solution)/shard_map/ppermute | solution.py:335
  23.6 23.6 %collective-permute-start.9 = (bf16[4,2,128,128]{3,2,1,0:T(8,128)(2,1)S(1)}, bf16[4,2,128,128]{3,2,1,0:T(8,128)(2,1)S(1)}, u32[]{:S(2)}, u32[]{:S(2)}) collective-permute-start(bf16[4,2,128,128]{3,2,1,0:T(8,128)(2,1)S(1)} %bitcast.19), channel_id=1, source_target_pairs={{0,1},{1,0},{2,3},{3,2},{4,5},{5,4},{6,7},{7,6},{8,9},{9,8},{10,11... | collective-permute-start | bytes 786440 | tf_op jit(solution)/shard_map/ppermute | solution.py:335
  29.3 8.3 %collective-permute-start.11 = (bf16[2,128,128]{2,1,0:T(8,128)(2,1)S(1)}, bf16[2,128,128]{2,1,0:T(8,128)(2,1)S(1)}, u32[]{:S(2)}, u32[]{:S(2)}) collective-permute-start(bf16[2,128,128]{2,1,0:T(8,128)(2,1)S(1)} %bitcast.21), channel_id=1, source_target_pairs={{0,3},{1,2},{2,5},{3,4},{4,7},{5,6},{6,9},{7,8},{8,11},{9,10},{10,... | collective-permute-start | bytes 196616 | tf_op jit(solution)/shard_map/ppermute | solution.py:335
  29.3 7.6 %collective-permute-start = (f32[1]{0:T(128)}, f32[1]{0:T(128)}, u32[]{:S(2)}, u32[]{:S(2)}) collective-permute-start(f32[1]{0:T(128)} %param.17), channel_id=1, source_target_pairs={{0,2},{1,3},{2,4},{3,5},{4,6},{5,7},{6,8},{7,9},{8,10},{9,11},{10,... | collective-permute-start | bytes 20 | tf_op jit(solution)/shard_map/ppermute | solution.py:335
  31.5 0.7 %copy-start.8 = (bf16[4,128,128]{2,1,0:T(8,128)(2,1)}, bf16[4,128,128]{2,1,0:T(8,128)(2,1)S(1)}, u32[]{:S(2)}) copy-start(bf16[4,128,128]{2,1,0:T(8,128)(2,1)S(1)} %collective-permute-done.5.refs_5_) | copy-start | bytes 393220
  36.2 10.9 %collective-permute-start.8 = (bf16[4,128,128]{2,1,0:T(8,128)(2,1)}, bf16[4,128,128]{2,1,0:T(8,128)(2,1)S(1)}, u32[]{:S(2)}, u32[]{:S(2)}) collective-permute-start(bf16[4,128,128]{2,1,0:T(8,128)(2,1)} %chain_last.1.refs_2_), channel_id=1, source_target_pairs={{0,1},{1,0},{2,3},{3,2},{4,5},{5,4},{6,7},{7,6},{8,9},{9,8},{10,11... | collective-permute-start | bytes 393224 | tf_op jit(solution)/shard_map/ppermute | solution.py:335
  36.9 10.3 %collective-permute-start.7 = (bf16[4,128,128]{2,1,0:T(8,128)(2,1)}, bf16[4,128,128]{2,1,0:T(8,128)(2,1)S(1)}, u32[]{:S(2)}, u32[]{:S(2)}) collective-permute-start(bf16[4,128,128]{2,1,0:T(8,128)(2,1)} %chain_last.1.refs_2_), channel_id=1, source_target_pairs={{0,3},{1,30},{2,5},{3,0},{4,7},{5,2},{6,9},{7,4},{8,11},{9,6},{10,... | collective-permute-start | bytes 393224 | tf_op jit(solution)/shard_map/ppermute | solution.py:335
  36.9 10.3 %collective-permute-start.6 = (bf16[4,128,128]{2,1,0:T(8,128)(2,1)}, bf16[4,128,128]{2,1,0:T(8,128)(2,1)S(1)}, u32[]{:S(2)}, u32[]{:S(2)}) collective-permute-start(bf16[4,128,128]{2,1,0:T(8,128)(2,1)} %chain_last.1.refs_2_), channel_id=1, source_target_pairs={{0,2},{1,31},{2,4},{3,1},{4,6},{5,3},{6,8},{7,5},{8,10},{9,7},{10,... | collective-permute-start | bytes 393224 | tf_op jit(solution)/shard_map/ppermute | solution.py:335
  37.6 9.7 %copy-start.10 = (bf16[2,128,128]{2,1,0:T(8,128)(2,1)}, bf16[2,128,128]{2,1,0:T(8,128)(2,1)S(1)}, u32[]{:S(2)}) copy-start(bf16[2,128,128]{2,1,0:T(8,128)(2,1)S(1)} %collective-permute-done.11.refs_8_) | copy-start | bytes 196612
  37.6 9.6 %collective-permute-start.10 = (bf16[2,128,128]{2,1,0:T(8,128)(2,1)S(1)}, bf16[2,128,128]{2,1,0:T(8,128)(2,1)S(1)}, u32[]{:S(2)}, u32[]{:S(2)}) collective-permute-start(bf16[2,128,128]{2,1,0:T(8,128)(2,1)S(1)} %bitcast.22), channel_id=1, source_target_pairs={{0,2},{1,3},{2,4},{3,5},{4,6},{5,7},{6,8},{7,9},{8,10},{9,11},{10,... | collective-permute-start | bytes 196616 | tf_op jit(solution)/shard_map/ppermute | solution.py:335
  47.2 0.6 %copy-start.11 = (bf16[2,128,128]{2,1,0:T(8,128)(2,1)}, bf16[2,128,128]{2,1,0:T(8,128)(2,1)S(1)}, u32[]{:S(2)}) copy-start(bf16[2,128,128]{2,1,0:T(8,128)(2,1)S(1)} %collective-permute-done.10.refs_7_) | copy-start | bytes 196612
  47.2 0.7 %copy-start.4 = (bf16[4,2,128,128]{3,2,1,0:T(8,128)(2,1)}, bf16[4,2,128,128]{3,2,1,0:T(8,128)(2,1)S(1)}, u32[]{:S(2)}) copy-start(bf16[4,2,128,128]{3,2,1,0:T(8,128)(2,1)S(1)} %collective-permute-done.9.refs_6_) | copy-start | bytes 786436
  47.2 0.8 %copy-start.5 = (bf16[4,128,128]{2,1,0:T(8,128)(2,1)}, bf16[4,128,128]{2,1,0:T(8,128)(2,1)S(1)}, u32[]{:S(2)}) copy-start(bf16[4,128,128]{2,1,0:T(8,128)(2,1)S(1)} %collective-permute-done.8.refs_3_) | copy-start | bytes 393220
  47.2 0.8 %copy-start.6 = (bf16[4,128,128]{2,1,0:T(8,128)(2,1)}, bf16[4,128,128]{2,1,0:T(8,128)(2,1)S(1)}, u32[]{:S(2)}) copy-start(bf16[4,128,128]{2,1,0:T(8,128)(2,1)S(1)} %collective-permute-done.7.refs_1_) | copy-start | bytes 393220
  47.2 0.8 %copy-start.7 = (bf16[4,128,128]{2,1,0:T(8,128)(2,1)}, bf16[4,128,128]{2,1,0:T(8,128)(2,1)S(1)}, u32[]{:S(2)}) copy-start(bf16[4,128,128]{2,1,0:T(8,128)(2,1)S(1)} %collective-permute-done.6.refs_0_) | copy-start | bytes 393220
